TPU v7x, 8 devices: a whole 2x2x1 slice. The times are simulated.
8 devices in a mesh: tp: 8 (over z, y, x, core).
Axes of the slice: x: 2, y: 2, z: 1, core: 2. Of those that a mesh axis runs over, the one named last changes fastest.
Arguments:
- hidden: bfloat16 [3, 4096, 4096], P(None, 'tp')
- labels: int32 [3, 4096], P(None, 'tp')
- loss_mask: int32 [3, 4096], P(None, 'tp')
- norm_gain: float32 [4096], replicated
- w_head: bfloat16 [4096, 32768], P(None, 'tp')
Outputs:
- output 1: float32 [], replicated
- output 2: bfloat16 [3, 4096, 4096], P(None, 'tp')
- output 3: bfloat16 [4096, 32768], P(None, 'tp')
- output 4: float32 [4096], replicated
All inputs are finite; a program needn't handle non-finite values.
Results may differ from a plain program's by a relative error of at most 0.00838527.
Values are sent between devices in bfloat16 or wider.
A program may use at most 1 GiB of HBM per device.

v0:
```python
import jax
import jax.numpy as jnp
from jax import lax
from jax.sharding import PartitionSpec as P, NamedSharding

NORM_EPS = 1e-6


def rms_norm(x_rows, norm_gain):
    inv_rms = lax.rsqrt(jnp.mean(x_rows * x_rows, axis=-1, keepdims=True) + NORM_EPS)
    return x_rows * inv_rms * norm_gain


def solution(mesh):
    n_shards = mesh.shape['tp']

    def device_step(hidden, labels, loss_mask, norm_gain, w_head):
        batch_size, seq_loc, model_width = hidden.shape
        v_loc = w_head.shape[1]
        norm_loc, norm_vjp = jax.vjp(rms_norm, hidden.astype(jnp.float32), norm_gain)
        hn_all = lax.all_gather(norm_loc.astype(jnp.bfloat16), 'tp', axis=1, tiled=True)
        label_all = lax.all_gather(labels, 'tp', axis=1, tiled=True)
        mask_all = lax.all_gather(loss_mask, 'tp', axis=1, tiled=True)
        logits = jnp.einsum('btd,dv->btv', hn_all, w_head, preferred_element_type=jnp.float32)
        row_max = lax.pmax(jnp.max(logits, axis=-1), 'tp')
        sum_exp = lax.psum(jnp.sum(jnp.exp(logits - row_max[..., None]), axis=-1), 'tp')
        col_start = lax.axis_index('tp') * v_loc
        is_label = (lax.broadcasted_iota(jnp.int32, (1, 1, v_loc), 2) + col_start) == label_all[..., None]
        label_logit = lax.psum(jnp.sum(jnp.where(is_label, logits, 0.0), axis=-1), 'tp')
        log_norm = row_max + jnp.log(sum_exp)
        tok_weight = mask_all.astype(jnp.float32)
        kept_count = jnp.sum(tok_weight)
        mean_loss = jnp.sum(tok_weight * (log_norm - label_logit)) / kept_count
        tok_scale = tok_weight / kept_count
        d_logits = ((jnp.exp(logits - log_norm[..., None]) - is_label.astype(jnp.float32)) * tok_scale[..., None]).astype(jnp.bfloat16)
        d_head = jnp.einsum('btd,btv->dv', hn_all, d_logits, preferred_element_type=jnp.float32).astype(jnp.bfloat16)
        dhn_part = jnp.einsum('btv,dv->btd', d_logits, w_head, preferred_element_type=jnp.float32).astype(jnp.bfloat16)
        received = lax.all_to_all(dhn_part.reshape(batch_size, n_shards, seq_loc, model_width), 'tp', 1, 1, tiled=True)
        d_norm = jnp.sum(received, axis=1, dtype=jnp.float32)
        d_x, d_gain = norm_vjp(d_norm)
        d_gain = lax.psum(d_gain, 'tp')
        return mean_loss, d_x.astype(jnp.bfloat16), d_head, d_gain

    return jax.shard_map(device_step, mesh=mesh, in_specs=(P(None, 'tp', None), P(None, 'tp'), P(None, 'tp'), P(), P(None, 'tp')), out_specs=(P(), P(None, 'tp', None), P(None, 'tp'), P()), check_vma=False)
```

profile of v0, /device:TPU:0, one launch (start us, length us, event | category | flops | bytes accessed | tf_op | source)
XLA Modules:
  0.0 2861.0 jit_solution(12603694999168581013)
XLA Ops:
  7.2 0.0 all-gather.2.cloned.1.call-start
  7.2 7.1 fusion.12
  14.3 0.0 copy-start.12
  14.3 0.6 copy-done.12
  14.9 0.0 copy-start.10
  14.9 0.6 copy-done.10
  15.5 11.7 fusion.9
  27.2 0.0 all-gather.2.cloned.1.call-update
  27.2 0.0 all-reduce.3.cloned.1.call-start
  27.3 13.9 all_gather.11
  41.2 0.6 iota_add_fusion
  41.8 427.6 %all-gather.2.cloned.1.call-done = bf16[3,4096,4096]{2,1,0:T(8,128)(2,1)} async-done(((bf16[3,512,4096]{2,1,0:T(8,128)(2,1)}), bf16[3,4096,4096]{2,1,0:T(8,128)(2,1)}) %all-gather.2.cloned.1.call-update) | async-done | bytes 100663312 | tf_op jit(solution)/shard_map/all_gather | solution.py:21
  469.4 0.0 copy-start.1
  469.4 0.0 copy-start.8
  469.4 446.9 %fusion.17 = (f32[3,4096]{1,0:T(4,128)S(1)}, f32[3,4096,4096]{1,2,0:T(8,128)}) fusion(bf16[3,4096,4096]{2,1,0:T(8,128)(2,1)} %all-gather.2.cloned.1.call-done, bf16[4096,4096]{1,0:T(8,128)(2,1)} %param.9), kind=kOutput, calls=%fused_computation.33 | convolution fusion | flops 412367192064 | bytes 335593472 | tf_op jit(solution)/shard_map/btd,dv->btv/dot_general | solution.py:24
  916.4 22.6 pmax.7
  938.9 0.0 copy-done.1
  938.9 0.0 copy-done.8
  939.0 0.0 copy-start.14
  939.0 61.8 %fusion = (f32[3,4096]{1,0:T(4,128)}, f32[3,4096]{1,0:T(4,128)}) fusion(f32[3,4096,4096]{1,2,0:T(8,128)} %get-tuple-element.14, s32[3,4096]{1,0:T(4,128)S(1)} %copy-done.1, s32[4096]{0:T(1024)S(1)} %copy-done.8, f32[3,4096]{1,0:T(4,128)S(1)} %pmax.7), kind=kLoop, calls=%fused_computation.2 | loop fusion | flops 251633664 | bytes 201539584 | tf_op jit(solution)/shard_map/reduce_sum | solution.py:29
  1000.8 0.0 all-reduce.3.cloned.1.call-update
  1000.8 0.0 copy-done.14
  1000.8 13.0 all_gather.9
  1013.8 31.2 %all-reduce.3.cloned.1.call-done = (f32[3,4096]{1,0:T(4,128)}, f32[3,4096]{1,0:T(4,128)}) async-done(((f32[3,4096]{1,0:T(4,128)}, f32[3,4096]{1,0:T(4,128)}), (f32[3,4096]{1,0:T(4,128)}, f32[3,4096]{1,0:T(4,128)})) %all-reduce.3.cloned.1.call-update) | async-done | bytes 98320 | tf_op jit(solution)/shard_map/psum | solution.py:26
  1045.0 1.5 convert_reduce_fusion.1
  1046.5 0.0 copy-start.3
  1046.5 0.7 convert_divide_fusion
  1047.2 0.0 copy-start.5
  1048.5 95.8 %fusion.26 = bf16[3,4096,4096]{1,2,0:T(8,128)(2,1)} fusion(f32[3,4096,4096]{1,2,0:T(8,128)} %get-tuple-element.14, f32[3,4096]{1,0:T(4,128)S(1)} %convert_divide_fusion, f32[3,4096]{1,0:T(4,128)S(1)} %get-tuple-element.12, s32[3,4096]{1,0:T(4,128)S(1)} %copy-done.1, s32[4096]{0:T(1024)S(1)} %copy-done.8), kind=kLoop, calls=%fused_computation.5.clone.1.clone.1 | loop fusion | flops 301989888 | bytes 302153728 | tf_op jit(solution)/shard_map/btv,dv->btd/dot_general | solution.py:37
  1144.3 0.0 copy-done.3
  1144.3 0.0 copy-done.5
  1144.3 433.6 %convolution_convert_fusion = bf16[3,4096,4096]{2,1,0:T(8,128)(2,1)} fusion(bf16[4096,4096]{1,0:T(8,128)(2,1)} %param.9, bf16[3,4096,4096]{1,2,0:T(8,128)(2,1)} %fusion.26), kind=kOutput, calls=%fused_computation.9 | convolution fusion | flops 412367192064 | bytes 234881024 | tf_op jit(solution)/shard_map/btv,dv->btd/dot_general | solution.py:37
  1577.9 65.2 %copy.15 = bf16[3,8,512,4096]{3,2,0,1:T(8,128)(2,1)} copy(bf16[3,8,512,4096]{3,2,1,0:T(8,128)(2,1)} %bitcast.2) | data formatting | bytes 201326592 | tf_op jit(solution)/shard_map/reshape | solution.py:38
  1643.1 0.0 copy-start.2
  1643.1 0.0 copy-start.4
  1643.1 0.0 copy-start.6
  1643.1 0.0 copy-start.9
  1643.1 11.2 all-to-all-start
  1654.3 0.0 copy-done.2
  1654.4 0.0 copy-done.4
  1654.4 0.0 copy-done.6
  1654.4 0.0 copy-done.9
  1654.4 479.3 %bitcast_convert_fusion = bf16[4096,4096]{1,0:T(8,128)(2,1)} fusion(bf16[3,4096,4096]{2,1,0:T(8,128)(2,1)} %all-gather.2.cloned.1.call-done, f32[3,4096,4096]{1,2,0:T(8,128)} %get-tuple-element.14, f32[3,4096]{1,0:T(4,128)S(1)} %copy-done.6, f32[3,4096]{1,0:T(4,128)S(1)} %copy-done.4, s32[3,4096]{1,0:T(4,128)S(1)} %copy-done.2, s32[4096]{0:T(1024)S(1)} %copy-done.9), kind=kOutput, calls=%fused_computation.8 | convolution fusion | flops 412635627520 | bytes 335708160 | tf_op jit(solution)/shard_map/btd,btv->dv/dot_general | solution.py:36
  2133.7 0.0 copy-start.7
  2133.7 0.0 copy-start.11
  2133.7 0.0 copy-start.13
  2133.7 604.3 %all-to-all-done = bf16[3,8,512,4096]{3,2,0,1:T(8,128)(2,1)} async-done(((bf16[3,8,512,4096]{3,2,0,1:T(8,128)(2,1)}), bf16[3,8,512,4096]{3,2,0,1:T(8,128)(2,1)}, u32[]{:S(2)}, u32[]{:S(2)}) %all-to-all-start) | async-done | bytes 100663328 | tf_op jit(solution)/shard_map/all_to_all | solution.py:38
  2738.0 0.0 copy-start
  2738.0 60.7 %convert_reduce_fusion = f32[3,512,4096]{2,1,0:T(8,128)} fusion(bf16[3,8,512,4096]{3,2,0,1:T(8,128)(2,1)} %all-to-all-done), kind=kLoop, calls=%fused_computation.6 | loop fusion | flops 94371840 | bytes 125829120 | tf_op jit(solution)/shard_map/reduce_sum | solution.py:39
  2798.7 0.0 copy-done.7
  2798.7 0.0 copy-done.11
  2798.7 0.0 copy-done
  2798.7 13.6 fusion.10
  2812.4 22.3 psum.23
  2834.7 0.0 copy-done.13
  2834.7 18.1 fusion.11
  (2 shorter events, 0.0 us)
Async XLA Ops:
  7.2 462.3 %all-gather.2.cloned.1.call-start = ((), (), s32[]{:S(2)}) async-start(), calls=%async_computation.1 | async-start | bytes 113246208 | tf_op jit(solution)/shard_map/all_gather | solution.py:21
  14.3 0.6 copy-start.12
  14.9 0.6 copy-start.10
  27.2 1017.7 %all-reduce.3.cloned.1.call-start = ((), (), s32[]{:S(2)}) async-start(), calls=%async_computation.2 | async-start | bytes 262144 | tf_op jit(solution)/shard_map/psum | solution.py:26
  469.4 469.5 %copy-start.1 = (s32[3,4096]{1,0:T(4,128)S(1)}, s32[3,4096]{1,0:T(4,128)}, u32[]{:S(2)}) copy-start(s32[3,4096]{1,0:T(4,128)} %all_gather.11) | copy-start | bytes 147460
  469.4 469.5 %copy-start.8 = (s32[4096]{0:T(1024)S(1)}, s32[4096]{0:T(1024)}, u32[]{:S(2)}) copy-start(s32[4096]{0:T(1024)} %iota_add_fusion) | copy-start | bytes 49156
  939.0 61.8 %copy-start.14 = (s32[3,512]{1,0:T(4,128)S(1)}, s32[3,512]{1,0:T(4,128)}, u32[]{:S(2)}) copy-start(s32[3,512]{1,0:T(4,128)} %param.7) | copy-start | bytes 18436
  1046.5 97.8 %copy-start.3 = (f32[3,4096]{1,0:T(4,128)}, f32[3,4096]{1,0:T(4,128)S(1)}, u32[]{:S(2)}) copy-start(f32[3,4096]{1,0:T(4,128)S(1)} %get-tuple-element.12) | copy-start | bytes 147460
  1047.2 97.1 %copy-start.5 = (f32[3,4096]{1,0:T(4,128)}, f32[3,4096]{1,0:T(4,128)S(1)}, u32[]{:S(2)}) copy-start(f32[3,4096]{1,0:T(4,128)S(1)} %convert_divide_fusion) | copy-start | bytes 147460
  1643.1 11.2 copy-start.2
  1643.1 11.2 copy-start.4
  1643.1 11.3 copy-start.6
  1643.1 11.2 copy-start.9
  1643.1 1094.9 %all-to-all-start = ((bf16[3,8,512,4096]{3,2,0,1:T(8,128)(2,1)}), bf16[3,8,512,4096]{3,2,0,1:T(8,128)(2,1)}, u32[]{:S(2)}, u32[]{:S(2)}) async-start(bf16[3,8,512,4096]{3,2,0,1:T(8,128)(2,1)} %copy.15), calls=%async_computation | async-start | bytes 201326592 | tf_op jit(solution)/shard_map/all_to_all | solution.py:38
  2133.7 665.1 %copy-start.7 = (f32[4096]{0:T(1024)S(1)}, f32[4096]{0:T(1024)}, u32[]{:S(2)}) copy-start(f32[4096]{0:T(1024)} %param.8) | copy-start | bytes 49156
  2133.7 665.1 %copy-start.11 = (f32[3,512]{1,0:T(4,128)S(1)}, f32[3,512]{1,0:T(4,128)}, u32[]{:S(2)}) copy-start(f32[3,512]{1,0:T(4,128)} %copy-done.10) | copy-start | bytes 18436
  2133.7 701.0 %copy-start.13 = (f32[3,512]{1,0:T(4,128)S(1)}, f32[3,512]{1,0:T(4,128)}, u32[]{:S(2)}) copy-start(f32[3,512]{1,0:T(4,128)} %copy-done.12) | copy-start | bytes 18436
  2738.0 60.7 %copy-start = (bf16[3,512,4096]{2,1,0:T(8,128)(2,1)S(1)}, bf16[3,512,4096]{2,1,0:T(8,128)(2,1)}, u32[]{:S(2)}) copy-start(bf16[3,512,4096]{2,1,0:T(8,128)(2,1)} %param.5) | copy-start | bytes 37748740
Sparse Core Ops, SparseCore 0:
  27.4 442.0 all-gather.1
  1000.9 44.0 all-reduce.2
where the time goes:
time: 2870 us; the launch traced here: 2860 us
  matrix products  1360 us (47%)
  waiting for transfers between devices  1060 us (37%)
  other arithmetic  272 us (9%)
  blocking collectives  71.7 us (2%)
  local copies, waits for them, and re-layouts  66.5 us (2%)
    all_to_all x1, waiting for transfers between devices, device_step(): lax.all_to_all(dhn_part.reshape(batch_size, n_shards, seq_loc, model_widt...  604 us
    dot_general x1, matrix products, device_step(): jnp.einsum('btd,btv->dv', hn_all, d_logits, preferred_element_type=jnp.fl...  479 us
    dot_general x1, matrix products, device_step(): jnp.einsum('btd,dv->btv', hn_all, w_head, preferred_element_type=jnp.floa...  447 us
    dot_general x1, matrix products, device_step(): jnp.einsum('btv,dv->btd', d_logits, w_head, preferred_element_type=jnp.fl...  434 us
    all_gather x1, waiting for transfers between devices, device_step(): lax.all_gather(norm_loc.astype(jnp.bfloat16), 'tp', axis=1, tiled=True)  428 us
    dot_general x1, other arithmetic, device_step(): jnp.einsum('btv,dv->btd', d_logits, w_head, preferred_element_type=jnp.fl...  95.8 us
    reshape x1, local copies, waits for them, and re-layouts, device_step(): dhn_part.reshape(batch_size, n_shards, seq_loc, model_width)  65.2 us
    reduce_sum x1, other arithmetic, device_step(): jnp.sum(jnp.where(is_label, logits, 0.0), axis=-1)  61.8 us
  transfers between devices with their start and end apart: 3, of which 3 were waited for; matrix products, arithmetic and copies ran while one was open for 17% of the time, Pallas kernels for 0%

commit v1 on v0

v1 whole, which is shorter than its diff:
```python
import jax
import jax.numpy as jnp
from jax import lax
from jax.sharding import PartitionSpec as P

NORM_EPS = 1e-6


def rms_norm(x_rows, norm_gain):
    inv_rms = lax.rsqrt(jnp.mean(x_rows * x_rows, axis=-1, keepdims=True) + NORM_EPS)
    return x_rows * inv_rms * norm_gain


def solution(mesh):
    n_shards = mesh.shape['tp']

    def device_step(hidden, labels, loss_mask, norm_gain, w_head):
        batch_size, seq_loc, model_width = hidden.shape
        v_loc = w_head.shape[1]
        f32 = jnp.float32
        targets = lax.all_gather(jnp.stack([labels, loss_mask]), 'tp', axis=2, tiled=True)
        label_all, mask_all = targets[0], targets[1]
        tok_weight = mask_all.astype(f32)
        kept_count = jnp.sum(tok_weight)
        tok_scale = tok_weight / kept_count
        col_start = lax.axis_index('tp') * v_loc
        loc_label = label_all - col_start

        hn = []
        for b in range(batch_size):
            norm_b = rms_norm(hidden[b].astype(f32), norm_gain).astype(jnp.bfloat16)
            hn.append(lax.all_gather(norm_b, 'tp', axis=0, tiled=True))

        col_ids = lax.broadcasted_iota(jnp.int32, (1, v_loc), 1)
        logits, maxes, sums, picked = [], [], [], []
        for b in range(batch_size):
            z = jnp.dot(hn[b], w_head, preferred_element_type=f32)
            m = jnp.max(z, axis=-1)
            logits.append(z)
            maxes.append(m)
            sums.append(jnp.sum(jnp.exp(z - m[:, None]), axis=-1))
            picked.append(jnp.sum(jnp.where(col_ids == loc_label[b][:, None], z, 0.0), axis=-1))
        stats = lax.all_gather(jnp.stack([jnp.stack(maxes), jnp.stack(sums)]), 'tp', axis=0)
        row_max = jnp.max(stats[:, 0], axis=0)
        sum_exp = jnp.sum(stats[:, 1] * jnp.exp(stats[:, 0] - row_max[None]), axis=0)
        log_norm = row_max + jnp.log(sum_exp)
        owned = (loc_label >= 0) & (loc_label < v_loc)
        loss_part = jnp.sum(jnp.where(owned, tok_weight * (log_norm - jnp.stack(picked)), 0.0))

        d_logits, reduced = [], []
        for b in range(batch_size):
            is_label = (col_ids == loc_label[b][:, None]).astype(f32)
            dz = ((jnp.exp(logits[b] - log_norm[b][:, None]) - is_label) * tok_scale[b][:, None]).astype(jnp.bfloat16)
            d_logits.append(dz)
            part = lax.dot_general(dz, w_head, (((1,), (1,)), ((), ())), preferred_element_type=f32)
            part = lax.reduce_precision(part, 8, 7)
            reduced.append(lax.psum_scatter(part, 'tp', scatter_dimension=0, tiled=True))
        d_head = jnp.zeros((), f32)
        for b in range(batch_size):
            d_head = d_head + lax.dot_general(hn[b], d_logits[b], (((0,), (0,)), ((), ())), preferred_element_type=f32)
        d_head = d_head.astype(jnp.bfloat16)

        d_x, d_gain = [], jnp.zeros((model_width,), f32)
        for b in range(batch_size):
            _, norm_vjp = jax.vjp(rms_norm, hidden[b].astype(f32), norm_gain)
            d_x_b, d_gain_b = norm_vjp(reduced[b])
            d_x.append(d_x_b.astype(jnp.bfloat16))
            d_gain = d_gain + d_gain_b
        tail = lax.psum(jnp.concatenate([d_gain, jnp.full((128,), loss_part / 128.0)]), 'tp')
        mean_loss = jnp.sum(tail[model_width:]) / kept_count
        return mean_loss, jnp.stack(d_x), d_head, tail[:model_width]

    return jax.shard_map(device_step, mesh=mesh, in_specs=(P(None, 'tp', None), P(None, 'tp'), P(None, 'tp'), P(), P(None, 'tp')), out_specs=(P(), P(None, 'tp', None), P(None, 'tp'), P()), check_vma=False)
```

time: 2870 us -> 2120 us (0.74)
  waiting for transfers between devices: 1060 us -> 372 us
  matrix products: 1360 us -> 1510 us
  other arithmetic: 272 us -> 156 us
  local copies, waits for them, and re-layouts: 66.5 us -> 3.98 us
    all_to_all x1 -> x0, waiting for transfers between devices: 604 us -> none  [device_step(): lax.all_to_all(dhn_part.reshape(batch_size, n_shards, seq_loc, model_widt...]
    all_gather x1 -> x3, waiting for transfers between devices: 428 us -> 141 us  [device_step(): hn.append(lax.all_gather(norm_b, 'tp', axis=0, tiled=True))]
    reduce_scatter x0 -> x3, waiting for transfers between devices: none -> 230 us  [device_step(): lax.psum_scatter(part, 'tp', scatter_dimension=0, tiled=True)]
    dot_general x3 -> x9, matrix products: 1360 us -> 1510 us  [the longest x3 548 us: device_step(): lax.dot_general(dz, w_head, (((1,), (1,)), ((), ())), preferred_element_t...]
    reshape x1 -> x0, local copies, waits for them, and re-layouts: 65.2 us -> none  [device_step(): dhn_part.reshape(batch_size, n_shards, seq_loc, model_width)]
    dot_general x1, other arithmetic: 95.8 us -> 34 us  [device_step(): lax.dot_general(hn[b], d_logits[b], (((0,), (0,)), ((), ())), preferred_e...]
    reduce_sum x2 -> x6, other arithmetic: 123 us -> 68.7 us  [the longest x3 66.5 us: device_step(): jnp.sum(jnp.where(col_ids == loc_label[b][:, None], z, 0.0), axis=-1)]
    psum x1 -> x0, waiting for transfers between devices: 31.2 us -> none  [device_step(): lax.psum(jnp.sum(jnp.exp(logits - row_max[..., None]), axis=-1), 'tp')]
  transfers between devices with their start and end apart: 3 -> 6, of which waited for: 3 -> 2; matrix products, arithmetic and copies ran while one was open for 17% -> 59% of each run, Pallas kernels for 0% -> 0%
where the time goes in v1:
time: 2120 us; the launch traced here: 2110 us
  matrix products  1510 us (71%)
  waiting for transfers between devices  372 us (18%)
  other arithmetic  156 us (7%)
  blocking collectives  51.5 us (2%)
    dot_general x3, matrix products, device_step(): lax.dot_general(dz, w_head, (((1,), (1,)), ((), ())), preferred_element_t...  548 us
    dot_general x3, matrix products, device_step(): lax.dot_general(hn[b], d_logits[b], (((0,), (0,)), ((), ())), preferred_e...  501 us
    dot_general x3, matrix products, device_step(): z = jnp.dot(hn[b], w_head, preferred_element_type=f32)  464 us
    reduce_scatter x3, waiting for transfers between devices, device_step(): lax.psum_scatter(part, 'tp', scatter_dimension=0, tiled=True)  230 us
    all_gather x3, waiting for transfers between devices, device_step(): hn.append(lax.all_gather(norm_b, 'tp', axis=0, tiled=True))  141 us
    reduce_sum x3, other arithmetic, device_step(): jnp.sum(jnp.where(col_ids == loc_label[b][:, None], z, 0.0), axis=-1)  66.5 us
  transfers between devices with their start and end apart: 6, of which 2 were waited for; matrix products, arithmetic and copies ran while one was open for 59% of the time, Pallas kernels for 0%

profile of v1, /device:TPU:0, one launch (start us, length us, event | category | flops | bytes accessed | tf_op | source)
XLA Modules:
  0.0 2114.2 jit_solution(3193447716189810924)
XLA Ops:
  7.2 0.0 all-gather.9.cloned.1.call-start
  7.2 6.0 fusion.15
  13.2 0.0 copy-start.26
  13.2 0.0 copy-start.30
  13.3 0.5 copy-done.28
  13.8 0.0 copy-done.26
  13.8 0.0 copy-done.30
  13.8 0.0 copy-done.20
  13.8 10.9 fusion.8
  24.7 0.0 copy-done.22
  24.7 0.0 all-gather.9.cloned.1.call-update
  24.7 0.0 all-gather.7.cloned.1.call-start
  24.8 0.7 all-gather.7.cloned.1.call-update
  25.5 0.0 all-gather.5.cloned.1.call-start
  25.5 0.7 all-gather.5.cloned.1.call-update
  26.2 0.0 reduce-scatter.4.cloned.1.call-start
  26.3 15.1 all_gather.23
  41.4 0.6 fusion.30
  42.0 0.6 fusion.38
  42.7 140.6 %all-gather.9.cloned.1.call-done = bf16[4096,4096]{1,0:T(8,128)(2,1)} async-done(((bf16[512,4096]{1,0:T(8,128)(2,1)}), bf16[4096,4096]{1,0:T(8,128)(2,1)}) %all-gather.9.cloned.1.call-update) | async-done | bytes 33554448 | tf_op jit(solution)/shard_map/all_gather | solution.py:32
  183.3 154.6 %fusion.39 = (f32[4096]{0:T(1024)S(1)}, f32[4096,4096]{0,1:T(8,128)}) fusion(bf16[4096,4096]{1,0:T(8,128)(2,1)} %all-gather.9.cloned.1.call-done, bf16[4096,4096]{1,0:T(8,128)(2,1)} %param.9), kind=kOutput, calls=%fused_computation.91 | convolution fusion | flops 137455730688 | bytes 134234112 | tf_op jit(solution)/shard_map/dot_general | solution.py:37
  337.9 22.4 %select_reduce_fusion = (f32[4096]{0:T(1024)}, f32[4096]{0:T(1024)}) fusion(f32[4096,4096]{0,1:T(8,128)} %get-tuple-element.42, s32[4096]{0:T(1024)S(1)} %bitcast.90, f32[4096]{0:T(1024)S(1)} %get-tuple-element.41), kind=kLoop, calls=%fused_computation.1 | loop fusion | flops 83877888 | bytes 67174400 | tf_op jit(solution)/shard_map/reduce_sum | solution.py:42
  360.3 154.6 %fusion.40 = (f32[4096]{0:T(1024)S(1)}, f32[4096,4096]{0,1:T(8,128)}) fusion(bf16[4096,4096]{1,0:T(8,128)(2,1)} %all-gather.7.cloned.1.call-done, bf16[4096,4096]{1,0:T(8,128)(2,1)} %param.9), kind=kOutput, calls=%fused_computation.92 | convolution fusion | flops 137455730688 | bytes 134234112 | tf_op jit(solution)/shard_map/dot_general | solution.py:37
  514.9 22.3 %select_reduce_fusion.1 = (f32[4096]{0:T(1024)}, f32[4096]{0:T(1024)}) fusion(f32[4096,4096]{0,1:T(8,128)} %get-tuple-element.44, s32[4096]{0:T(1024)S(1)} %bitcast.102, f32[4096]{0:T(1024)S(1)} %get-tuple-element.43), kind=kLoop, calls=%fused_computation.2 | loop fusion | flops 83877888 | bytes 67174400 | tf_op jit(solution)/shard_map/reduce_sum | solution.py:42
  537.3 155.1 %fusion.41 = (f32[4096]{0:T(1024)S(1)}, f32[4096,4096]{0,1:T(8,128)}) fusion(bf16[4096,4096]{1,0:T(8,128)(2,1)} %all-gather.5.cloned.1.call-done, bf16[4096,4096]{1,0:T(8,128)(2,1)} %param.9), kind=kOutput, calls=%fused_computation.93 | convolution fusion | flops 137455730688 | bytes 134234112 | tf_op jit(solution)/shard_map/dot_general | solution.py:37
  692.5 0.0 copy-start.5
  692.5 0.0 copy-start.6
  692.5 21.8 %select_reduce_fusion.2 = (f32[4096]{0:T(1024)S(1)}, f32[4096]{0:T(1024)S(1)}) fusion(f32[4096,4096]{0,1:T(8,128)} %get-tuple-element.46, s32[4096]{0:T(1024)S(1)} %bitcast.105, f32[4096]{0:T(1024)S(1)} %get-tuple-element.45), kind=kLoop, calls=%fused_computation.3 | loop fusion | flops 83877888 | bytes 67174400 | tf_op jit(solution)/shard_map/reduce_sum | solution.py:42
  714.5 14.0 all-gather
  728.5 0.1 bitcast_reduce_fusion
  728.6 0.2 fusion.25
  728.9 1.4 fusion.29
  730.3 0.6 fusion.37
  730.9 0.7 fusion.36
  731.6 182.6 %convolution_reduce-precision_fusion.2 = f32[4096,4096]{1,0:T(8,128)} fusion(bf16[4096,4096]{1,0:T(8,128)(2,1)} %param.9, f32[4096,4096]{0,1:T(8,128)} %get-tuple-element.46, f32[4096]{0:T(1024)S(1)} %bitcast.116, s32[4096]{0:T(1024)S(1)} %bitcast.106, f32[4096]{0:T(1024)S(1)} %bitcast.118), kind=kOutput, calls=%fused_computation.15 | convolution fusion | flops 137556393984 | bytes 167821312 | tf_op jit(solution)/shard_map/dot_general | solution.py:55
  914.2 0.0 copy-start.18
  914.2 0.0 reduce-scatter.4.cloned.1.call-update
  914.3 0.0 reduce-scatter.8.cloned.1.call-start
  914.3 0.6 copy-done.4
  914.9 0.0 copy-done.18
  914.9 0.0 copy-done.19
  915.0 182.7 %convolution_reduce-precision_fusion = f32[4096,4096]{1,0:T(8,128)} fusion(bf16[4096,4096]{1,0:T(8,128)(2,1)} %param.9, f32[4096,4096]{0,1:T(8,128)} %get-tuple-element.42, f32[4096]{0:T(1024)S(1)} %bitcast.108, s32[4096]{0:T(1024)S(1)} %bitcast.91, f32[4096]{0:T(1024)S(1)} %bitcast.110), kind=kOutput, calls=%fused_computation.13 | convolution fusion | flops 137556393984 | bytes 167821312 | tf_op jit(solution)/shard_map/dot_general | solution.py:55
  1097.7 0.0 reduce-scatter.8.cloned.1.call-update
  1097.7 0.0 copy-start.14
  1097.7 0.0 copy-start.32
  1097.7 0.0 reduce-scatter.6.cloned.1.call-start
  1097.8 34.0 %multiply_convert_fusion.15 = bf16[4096,4096]{0,1:T(8,128)(2,1)} fusion(f32[4096,4096]{0,1:T(8,128)} %get-tuple-element.42, f32[4096]{0:T(1024)S(1)} %bitcast.109, s32[4096]{0:T(1024)S(1)} %bitcast.92, f32[4096]{0:T(1024)S(1)} %bitcast.111), kind=kLoop, calls=%fused_computation.4.clone.clone.1 | loop fusion | flops 100663296 | bytes 100712448 | tf_op jit(solution)/shard_map/dot_general | solution.py:60
  1131.8 182.5 %convolution_reduce-precision_fusion.1 = f32[4096,4096]{1,0:T(8,128)} fusion(bf16[4096,4096]{1,0:T(8,128)(2,1)} %param.9, f32[4096,4096]{0,1:T(8,128)} %get-tuple-element.44, f32[4096]{0:T(1024)S(1)} %bitcast.112, s32[4096]{0:T(1024)S(1)} %bitcast.103, f32[4096]{0:T(1024)S(1)} %bitcast.114), kind=kOutput, calls=%fused_computation.14 | convolution fusion | flops 137556393984 | bytes 167821312 | tf_op jit(solution)/shard_map/dot_general | solution.py:55
  1314.4 0.0 reduce-scatter.6.cloned.1.call-update
  1315.0 0.0 copy-done.17
  1315.1 0.0 copy-done.37
  1315.1 0.0 copy-done.39
  1315.1 170.7 %fusion.34 = f32[4096,4096]{1,0:T(8,128)} fusion(bf16[4096,4096]{1,0:T(8,128)(2,1)} %all-gather.5.cloned.1.call-done, f32[4096,4096]{0,1:T(8,128)} %get-tuple-element.46, f32[4096]{0:T(1024)S(1)} %bitcast.117, s32[4096]{0:T(1024)S(1)} %bitcast.107, f32[4096]{0:T(1024)S(1)} %bitcast.119), kind=kOutput, calls=%fused_computation.86 | convolution fusion | flops 137539616768 | bytes 167821312 | tf_op jit(solution)/shard_map/dot_general | solution.py:60
  1485.8 170.2 %fusion.35 = f32[4096,4096]{1,0:T(8,128)} fusion(bf16[4096,4096]{1,0:T(8,128)(2,1)} %all-gather.7.cloned.1.call-done, f32[4096,4096]{0,1:T(8,128)} %get-tuple-element.44, f32[4096]{0:T(1024)S(1)} %bitcast.113, s32[4096]{0:T(1024)S(1)} %bitcast.104, f32[4096]{0:T(1024)S(1)} %bitcast.115), kind=kOutput, calls=%fused_computation.87 | convolution fusion | flops 137539616768 | bytes 167821312 | tf_op jit(solution)/shard_map/dot_general | solution.py:60
  1656.0 159.8 %add_convert_fusion = bf16[4096,4096]{1,0:T(8,128)(2,1)} fusion(f32[4096,4096]{1,0:T(8,128)} %fusion.34, f32[4096,4096]{1,0:T(8,128)} %fusion.35, bf16[4096,4096]{1,0:T(8,128)(2,1)} %all-gather.9.cloned.1.call-done, bf16[4096,4096]{0,1:T(8,128)(2,1)} %multiply_convert_fusion.15), kind=kOutput, calls=%fused_computation | convolution fusion | flops 137489285120 | bytes 234881024 | tf_op jit(solution)/shard_map/dot_general | solution.py:60
  1815.8 0.0 reduce-scatter.4.cloned.1.call-done
  1815.8 0.0 reduce-scatter.8.cloned.1.call-done
  1815.9 229.8 %reduce-scatter.6.cloned.1.call-done = f32[512,4096]{1,0:T(8,128)} async-done(((f32[4096,4096]{1,0:T(8,128)}), f32[512,4096]{1,0:T(8,128)}) %reduce-scatter.6.cloned.1.call-update) | async-done | bytes 8388624 | tf_op jit(solution)/shard_map/reduce_scatter | solution.py:57
  2045.7 15.6 fusion.16
  2061.3 22.4 %psum.7 = f32[4224]{0:T(1024)S(1)} all-reduce(f32[4224]{0:T(1024)S(1)} %concatenate.3), channel_id=1, replica_groups=mesh['tp'=8] {'tp'}, use_global_device_ids=true, to_apply=%region_22.23 | all-reduce | flops 4224 | bytes 33792 | tf_op jit(solution)/shard_map/psum | solution.py:69
  2083.7 0.6 slice_reduce_fusion
  2084.3 0.6 slice.96
  2086.3 14.2 fusion.23
  2100.6 5.5 pad_maximum_fusion
  (80 shorter events, 0.3 us)
Async XLA Ops:
  7.2 19.1 copy-start.40
  7.2 19.1 copy-start.41
  7.2 176.1 %all-gather.9.cloned.1.call-start = ((), (), s32[]{:S(2)}) async-start(), calls=%async_computation.5 | async-start | bytes 37748736 | tf_op jit(solution)/shard_map/all_gather | solution.py:32
  13.2 0.6 copy-start.28
  13.2 0.6 copy-start.26
  13.2 0.6 copy-start.30
  13.2 0.6 copy-start.20
  13.8 10.9 copy-start.22
  13.8 10.9 copy-start.24
  24.7 335.6 %all-gather.7.cloned.1.call-start = ((), (), s32[]{:S(2)}) async-start(), calls=%async_computation.4 | async-start | bytes 37748736 | tf_op jit(solution)/shard_map/all_gather | solution.py:32
  25.5 511.8 %all-gather.5.cloned.1.call-start = ((), (), s32[]{:S(2)}) async-start(), calls=%async_computation.3 | async-start | bytes 37748736 | tf_op jit(solution)/shard_map/all_gather | solution.py:32
  26.2 1789.6 %reduce-scatter.4.cloned.1.call-start = ((), (), s32[]{:S(2)}) async-start(), calls=%async_computation.6 | async-start | bytes 75497472 | tf_op jit(solution)/shard_map/reduce_scatter | solution.py:57
  41.4 296.5 %copy-start = (s32[2,3,4096]{2,1,0:T(4,128)}, s32[2,3,4096]{2,1,0:T(4,128)S(1)}, u32[]{:S(2)}) copy-start(s32[2,3,4096]{2,1,0:T(4,128)S(1)} %all_gather.23) | copy-start | bytes 294916
  183.3 154.6 %copy-start.3 = (s32[1,1,4096]{2,1,0:T(1,128)S(1)}, s32[1,1,4096]{2,1,0:T(1,128)}, u32[]{:S(2)}) copy-start(s32[1,1,4096]{2,1,0:T(1,128)} %get-tuple-element.39) | copy-start | bytes 49156
  337.9 22.4 %copy-start.7 = (f32[4096]{0:T(1024)}, f32[4096]{0:T(1024)S(1)}, u32[]{:S(2)}) copy-start(f32[4096]{0:T(1024)S(1)} %get-tuple-element.41) | copy-start | bytes 49156
  360.3 154.6 %copy-start.13 = (s32[1,1,4096]{2,1,0:T(1,128)S(1)}, s32[1,1,4096]{2,1,0:T(1,128)}, u32[]{:S(2)}) copy-start(s32[1,1,4096]{2,1,0:T(1,128)} %get-tuple-element.38) | copy-start | bytes 49156
  514.9 22.4 %copy-start.10 = (f32[4096]{0:T(1024)}, f32[4096]{0:T(1024)S(1)}, u32[]{:S(2)}) copy-start(f32[4096]{0:T(1024)S(1)} %get-tuple-element.43) | copy-start | bytes 49156
  537.3 155.2 %copy-start.16 = (s32[1,1,4096]{2,1,0:T(1,128)S(1)}, s32[1,1,4096]{2,1,0:T(1,128)}, u32[]{:S(2)}) copy-start(s32[1,1,4096]{2,1,0:T(1,128)} %get-tuple-element.40) | copy-start | bytes 49156
  692.4 21.9 %copy-start.9 = (f32[4096]{0:T(1024)S(1)}, f32[4096]{0:T(1024)}, u32[]{:S(2)}) copy-start(f32[4096]{0:T(1024)} %get-tuple-element.9) | copy-start | bytes 49156
  692.4 21.9 %copy-start.12 = (f32[4096]{0:T(1024)S(1)}, f32[4096]{0:T(1024)}, u32[]{:S(2)}) copy-start(f32[4096]{0:T(1024)} %get-tuple-element.7) | copy-start | bytes 49156
  692.4 22.0 %copy-start.8 = (f32[4096]{0:T(1024)S(1)}, f32[4096]{0:T(1024)}, u32[]{:S(2)}) copy-start(f32[4096]{0:T(1024)} %copy-done.7) | copy-start | bytes 49156
  692.4 22.0 %copy-start.11 = (f32[4096]{0:T(1024)S(1)}, f32[4096]{0:T(1024)}, u32[]{:S(2)}) copy-start(f32[4096]{0:T(1024)} %copy-done.10) | copy-start | bytes 49156
  692.4 36.4 %copy-start.1 = (s32[2,3,4096]{2,1,0:T(4,128)S(1)}, s32[2,3,4096]{2,1,0:T(4,128)}, u32[]{:S(2)}) copy-start(s32[2,3,4096]{2,1,0:T(4,128)} %copy-done) | copy-start | bytes 294916
  692.5 36.4 %copy-start.5 = (f32[4096]{0:T(1024)S(1)}, f32[4096]{0:T(1024)}, u32[]{:S(2)}) copy-start(f32[4096]{0:T(1024)} %get-tuple-element.8) | copy-start | bytes 49156
  692.5 36.4 %copy-start.6 = (f32[4096]{0:T(1024)S(1)}, f32[4096]{0:T(1024)}, u32[]{:S(2)}) copy-start(f32[4096]{0:T(1024)} %get-tuple-element.6) | copy-start | bytes 49156
  730.9 183.3 %copy-start.36 = (f32[1,4096]{1,0:T(1,128)}, f32[1,4096]{1,0:T(1,128)S(1)}, u32[]{:S(2)}) copy-start(f32[1,4096]{1,0:T(1,128)S(1)} %get-tuple-element.37) | copy-start | bytes 49156
  731.6 182.7 %copy-start.38 = (f32[1,4096]{1,0:T(1,128)}, f32[1,4096]{1,0:T(1,128)S(1)}, u32[]{:S(2)}) copy-start(f32[1,4096]{1,0:T(1,128)S(1)} %get-tuple-element.34) | copy-start | bytes 49156
  914.2 0.7 copy-start.4
  914.2 0.7 copy-start.18
  914.2 0.7 copy-start.19
  914.3 901.6 %reduce-scatter.8.cloned.1.call-start = ((), (), s32[]{:S(2)}) async-start(), calls=%async_computation.8 | async-start | bytes 75497472 | tf_op jit(solution)/shard_map/reduce_scatter | solution.py:57
  1097.7 34.1 %copy-start.14 = (s32[1,1,4096]{2,1,0:T(1,128)S(1)}, s32[1,1,4096]{2,1,0:T(1,128)}, u32[]{:S(2)}) copy-start(s32[1,1,4096]{2,1,0:T(1,128)} %get-tuple-element.38) | copy-start | bytes 49156
  1097.7 34.1 %copy-start.32 = (f32[1,4096]{1,0:T(1,128)S(1)}, f32[1,4096]{1,0:T(1,128)}, u32[]{:S(2)}) copy-start(f32[1,4096]{1,0:T(1,128)} %get-tuple-element.35) | copy-start | bytes 49156
  1097.7 34.1 %copy-start.34 = (f32[1,4096]{1,0:T(1,128)S(1)}, f32[1,4096]{1,0:T(1,128)}, u32[]{:S(2)}) copy-start(f32[1,4096]{1,0:T(1,128)} %get-tuple-element.32) | copy-start | bytes 49156
  1097.7 947.9 %reduce-scatter.6.cloned.1.call-start = ((), (), s32[]{:S(2)}) async-start(), calls=%async_computation.7 | async-start | bytes 75497472 | tf_op jit(solution)/shard_map/reduce_scatter | solution.py:57
  1314.3 0.7 copy-start.17
  1314.3 0.7 copy-start.37
  1314.3 0.7 copy-start.39
  1315.1 170.7 %copy-start.15 = (s32[1,1,4096]{2,1,0:T(1,128)S(1)}, s32[1,1,4096]{2,1,0:T(1,128)}, u32[]{:S(2)}) copy-start(s32[1,1,4096]{2,1,0:T(1,128)} %get-tuple-element.38) | copy-start | bytes 49156
  1315.1 170.7 %copy-start.33 = (f32[1,4096]{1,0:T(1,128)S(1)}, f32[1,4096]{1,0:T(1,128)}, u32[]{:S(2)}) copy-start(f32[1,4096]{1,0:T(1,128)} %get-tuple-element.35) | copy-start | bytes 49156
  1315.1 170.7 %copy-start.35 = (f32[1,4096]{1,0:T(1,128)S(1)}, f32[1,4096]{1,0:T(1,128)}, u32[]{:S(2)}) copy-start(f32[1,4096]{1,0:T(1,128)} %get-tuple-element.32) | copy-start | bytes 49156
  1656.0 389.6 %copy-start.2 = (f32[4096]{0:T(1024)S(1)}, f32[4096]{0:T(1024)}, u32[]{:S(2)}) copy-start(f32[4096]{0:T(1024)} %param.8) | copy-start | bytes 49156
  1656.0 389.6 %copy-start.21 = (f32[512]{0:T(512)S(1)}, f32[512]{0:T(512)}, u32[]{:S(2)}) copy-start(f32[512]{0:T(512)} %copy-done.20) | copy-start | bytes 6148
  1656.0 389.6 %copy-start.23 = (f32[512]{0:T(512)S(1)}, f32[512]{0:T(512)}, u32[]{:S(2)}) copy-start(f32[512]{0:T(512)} %copy-done.22) | copy-start | bytes 6148
  1656.0 389.6 %copy-start.25 = (f32[512]{0:T(512)S(1)}, f32[512]{0:T(512)}, u32[]{:S(2)}) copy-start(f32[512]{0:T(512)} %copy-done.24) | copy-start | bytes 6148
  1815.8 270.5 %copy-start.27 = (f32[512]{0:T(512)S(1)}, f32[512]{0:T(512)}, u32[]{:S(2)}) copy-start(f32[512]{0:T(512)} %copy-done.26) | copy-start | bytes 6148
  1815.8 270.5 %copy-start.29 = (f32[512]{0:T(512)S(1)}, f32[512]{0:T(512)}, u32[]{:S(2)}) copy-start(f32[512]{0:T(512)} %copy-done.28) | copy-start | bytes 6148
  1815.8 270.5 %copy-start.31 = (f32[512]{0:T(512)S(1)}, f32[512]{0:T(512)}, u32[]{:S(2)}) copy-start(f32[512]{0:T(512)} %copy-done.30) | copy-start | bytes 6148
Sparse Core Ops, SparseCore 0:
  24.8 158.3 all-gather.8
  185.6 155.2 all-gather.6
  342.7 155.2 all-gather.4
  914.4 375.0 reduce-scatter.3
  1292.8 374.6 reduce-scatter.7
  1670.9 374.6 reduce-scatter.5

commit v2 on v0

v2 whole, which is shorter than its diff:
```python
import jax
import jax.numpy as jnp
from jax import lax
from jax.sharding import PartitionSpec as P

NORM_EPS = 1e-6


def rms_norm(x_rows, norm_gain):
    inv_rms = lax.rsqrt(jnp.mean(x_rows * x_rows, axis=-1, keepdims=True) + NORM_EPS)
    return x_rows * inv_rms * norm_gain


def solution(mesh):
    n_shards = mesh.shape['tp']

    def device_step(hidden, labels, loss_mask, norm_gain, w_head):
        batch_size, seq_loc, model_width = hidden.shape
        v_loc = w_head.shape[1]
        f32 = jnp.float32
        lead = seq_loc // 4
        chunks = [(0, 0, lead), (0, lead, seq_loc)] + [(b, 0, seq_loc) for b in range(1, batch_size)]

        x_loc = [hidden[b, lo:hi].astype(f32) for b, lo, hi in chunks]
        hn = []
        for x in x_loc:
            hn.append(lax.all_gather(rms_norm(x, norm_gain).astype(jnp.bfloat16), 'tp', axis=0, tiled=True))

        targets = lax.all_gather(jnp.stack([labels, loss_mask]), 'tp', axis=0)
        col_start = lax.axis_index('tp') * v_loc
        loc_label_all = targets[:, 0] - col_start
        tok_weight_all = targets[:, 1].astype(f32)
        kept_count = jnp.sum(tok_weight_all)
        col_ids = lax.broadcasted_iota(jnp.int32, (1, v_loc), 1)

        loss_part = jnp.zeros((), f32)
        d_logits, reduced = [], []
        part = None
        for i, (b, lo, hi) in enumerate(chunks):
            loc_label = loc_label_all[:, b, lo:hi].reshape(-1)
            tok_weight = tok_weight_all[:, b, lo:hi].reshape(-1)
            h = hn[i]
            if part is not None:
                h, _ = lax.optimization_barrier((h, part))
            z = jnp.dot(h, w_head, preferred_element_type=f32)
            m = jnp.max(z, axis=-1)
            s = jnp.sum(jnp.exp(z - m[:, None]), axis=-1)
            picked = jnp.sum(jnp.where(col_ids == loc_label[:, None], z, 0.0), axis=-1)
            stats = lax.all_gather(jnp.stack([m, s]), 'tp', axis=0)
            row_max = jnp.max(stats[:, 0], axis=0)
            log_norm = row_max + jnp.log(jnp.sum(stats[:, 1] * jnp.exp(stats[:, 0] - row_max[None]), axis=0))
            owned = (loc_label >= 0) & (loc_label < v_loc)
            loss_part = loss_part + jnp.sum(jnp.where(owned, tok_weight * (log_norm - picked), 0.0))
            is_label = (col_ids == loc_label[:, None]).astype(f32)
            dz = ((jnp.exp(z - log_norm[:, None]) - is_label) * (tok_weight / kept_count)[:, None]).astype(jnp.bfloat16)
            dz = lax.optimization_barrier(dz)
            d_logits.append(dz)
            part = lax.dot_general(dz, w_head, (((1,), (1,)), ((), ())), preferred_element_type=f32)
            part = lax.reduce_precision(part, 8, 7)
            reduced.append(lax.psum_scatter(part, 'tp', scatter_dimension=0, tiled=True))
        hn_late, dz_late, _ = lax.optimization_barrier((hn, d_logits, part))
        d_head = jnp.zeros((), f32)
        for h, dz in zip(hn_late, dz_late):
            d_head = d_head + lax.dot_general(h, dz, (((0,), (0,)), ((), ())), preferred_element_type=f32)
        d_head = d_head.astype(jnp.bfloat16)

        d_x, d_gain = [], jnp.zeros((model_width,), f32)
        for x, d_norm in zip(x_loc, reduced):
            _, norm_vjp = jax.vjp(rms_norm, x, norm_gain)
            d_x_i, d_gain_i = norm_vjp(d_norm)
            d_x.append(d_x_i.astype(jnp.bfloat16))
            d_gain = d_gain + d_gain_i
        tail = lax.psum(jnp.concatenate([d_gain, jnp.full((128,), loss_part / 128.0)]), 'tp')
        mean_loss = jnp.sum(tail[model_width:]) / kept_count
        d_hidden = jnp.zeros(hidden.shape, jnp.bfloat16)
        for (b, lo, hi), d_x_i in zip(chunks, d_x):
            d_hidden = lax.dynamic_update_slice(d_hidden, d_x_i[None], (b, lo, 0))
        return mean_loss, d_hidden, d_head, tail[:model_width]

    return jax.shard_map(device_step, mesh=mesh, in_specs=(P(None, 'tp', None), P(None, 'tp'), P(None, 'tp'), P(), P(None, 'tp')), out_specs=(P(), P(None, 'tp', None), P(None, 'tp'), P()), check_vma=False)
```

time: 2870 us -> 1820 us (0.63)
  waiting for transfers between devices: 1060 us -> 23.7 us
  matrix products: 1360 us -> 1420 us
  local copies, waits for them, and re-layouts: 66.5 us -> 12.7 us
    all_to_all x1 -> x0, waiting for transfers between devices: 604 us -> none  [device_step(): lax.all_to_all(dhn_part.reshape(batch_size, n_shards, seq_loc, model_widt...]
    all_gather x1 -> x4, waiting for transfers between devices: 428 us -> 23 us  [device_step(): lax.all_gather(rms_norm(x, norm_gain).astype(jnp.bfloat16), 'tp', axis=0,...]
    dot_general x1 -> x0, other arithmetic: 95.8 us -> none  [device_step(): jnp.einsum('btv,dv->btd', d_logits, w_head, preferred_element_type=jnp.fl...]
    convert_element_type x2 -> x8, other arithmetic: 29.9 us -> 115 us  [the longest x4 101 us: device_step(): ((jnp.exp(z - log_norm[:, None]) - is_label) * (tok_weight / kept_count)[...]
    reshape x1 -> x0, local copies, waits for them, and re-layouts: 65.2 us -> none  [device_step(): dhn_part.reshape(batch_size, n_shards, seq_loc, model_width)]
    dot_general x3 -> x12, matrix products: 1360 us -> 1420 us  [the longest x4 496 us: device_step(): lax.dot_general(h, dz, (((0,), (0,)), ((), ())), preferred_element_type=f32)]
    reduce_sum x3 -> x13, other arithmetic: 124 us -> 79.7 us  [the longest x4 73.1 us: device_step(): picked = jnp.sum(jnp.where(col_ids == loc_label[:, None], z, 0.0), axis=-1)]
    all_gather x2 -> x5, blocking collectives: 26.9 us -> 65.8 us  [the longest x4 50.7 us: device_step(): stats = lax.all_gather(jnp.stack([m, s]), 'tp', axis=0)]
  transfers between devices with their start and end apart: 3 -> 8, of which waited for: 3 -> 2; matrix products, arithmetic and copies ran while one was open for 17% -> 91% of each run, Pallas kernels for 0% -> 0%
where the time goes in v2:
time: 1820 us; the launch traced here: 1810 us
  matrix products  1420 us (78%)
  other arithmetic  247 us (14%)
  blocking collectives  88.4 us (5%)
  waiting for transfers between devices  23.7 us (1%)
  between operations  20 us (1%)
    dot_general x4, matrix products, device_step(): lax.dot_general(h, dz, (((0,), (0,)), ((), ())), preferred_element_type=f32)  496 us
    dot_general x4, matrix products, device_step(): z = jnp.dot(h, w_head, preferred_element_type=f32)  465 us
    dot_general x4, matrix products, device_step(): lax.dot_general(dz, w_head, (((1,), (1,)), ((), ())), preferred_element_t...  457 us
    convert_element_type x4, other arithmetic, device_step(): ((jnp.exp(z - log_norm[:, None]) - is_label) * (tok_weight / kept_count)[...  101 us
    reduce_sum x4, other arithmetic, device_step(): picked = jnp.sum(jnp.where(col_ids == loc_label[:, None], z, 0.0), axis=-1)  73.1 us
    all_gather x4, blocking collectives, device_step(): stats = lax.all_gather(jnp.stack([m, s]), 'tp', axis=0)  50.7 us
  transfers between devices with their start and end apart: 8, of which 2 were waited for; matrix products, arithmetic and copies ran while one was open for 91% of the time, Pallas kernels for 0%

profile of v2, /device:TPU:0, one launch (start us, length us, event | category | flops | bytes accessed | tf_op | source)
XLA Modules:
  0.0 1810.0 jit_solution(14691607328774204931)
XLA Ops:
  7.2 1.5 fusion.32
  8.7 0.5 copy-done.29
  9.3 0.5 copy-done.27
  9.8 2.5 fusion.29
  12.4 2.6 fusion.19
  15.0 0.6 copy-done.19
  15.6 0.5 copy-done.13
  16.1 4.6 fusion.16
  20.8 4.4 fusion.10
  25.2 0.6 copy-done.21
  25.8 7.2 fusion.6
  33.1 15.0 all-gather.1
  48.2 0.6 fusion.46
  48.9 15.6 all-gather.14.cloned.1.call-done
  64.5 41.3 %fusion.68 = (f32[1024]{0:T(1024)S(1)}, f32[1024,4096]{1,0:T(8,128)S(1)}) fusion(bf16[1024,4096]{1,0:T(8,128)(2,1)} %all-gather.14.cloned.1.call-done, bf16[4096,4096]{1,0:T(8,128)(2,1)} %param.9), kind=kOutput, calls=%fused_computation.150 | convolution fusion | flops 34363932672 | bytes 58724352 | tf_op jit(solution)/shard_map/dot_general | solution.py:45
  105.8 5.6 select_reduce_fusion.3
  111.5 12.1 all-gather.5
  123.6 1.3 fusion.54
  124.9 7.9 multiply_convert_fusion.3
  132.8 43.2 %convolution_reduce-precision_fusion.3 = f32[1024,4096]{1,0:T(8,128)} fusion(bf16[1024,4096]{1,0:T(8,128)(2,1)} %multiply_convert_fusion.3, bf16[4096,4096]{1,0:T(8,128)(2,1)} %param.9), kind=kOutput, calls=%fused_computation.39 | convolution fusion | flops 34363932672 | bytes 58720256 | tf_op jit(solution)/shard_map/dot_general | solution.py:58
  176.1 0.5 all-gather.20.cloned.1.call-update
  176.6 0.3 reduce-scatter.7.cloned.1.call-start
  176.9 0.6 slice.108
  177.5 1.3 slice_divide_fusion.1
  178.8 0.6 fusion.66
  179.4 7.4 all-gather.16.cloned.1.call-done
  186.8 114.3 %fusion.69 = (f32[3072]{0:T(1024)S(1)}, f32[3072,4096]{1,0:T(8,128)}) fusion(bf16[3072,4096]{1,0:T(8,128)(2,1)} %all-gather.16.cloned.1.call-done, bf16[4096,4096]{1,0:T(8,128)(2,1)} %param.9), kind=kOutput, calls=%fused_computation.151 | convolution fusion | flops 103091798016 | bytes 109064192 | tf_op jit(solution)/shard_map/dot_general | solution.py:45
  301.1 24.0 %select_reduce_fusion.2 = (f32[3072]{0:T(1024)S(1)}, f32[3072]{0:T(1024)S(1)}) fusion(f32[3072,4096]{1,0:T(8,128)} %get-tuple-element.80, s32[3072]{0:T(1024)S(1)} %bitcast.164, f32[3072]{0:T(1024)S(1)} %get-tuple-element.79), kind=kLoop, calls=%fused_computation.9 | loop fusion | flops 62908416 | bytes 50380800 | tf_op jit(solution)/shard_map/reduce_sum | solution.py:48
  325.1 13.0 all-gather.6
  338.4 2.1 fusion.53
  340.5 25.9 %multiply_convert_fusion.2 = bf16[3072,4096]{1,0:T(8,128)(2,1)} fusion(f32[3072,4096]{1,0:T(8,128)} %get-tuple-element.80, f32[3072]{0:T(1024)S(1)} %bitcast.176, s32[3072]{0:T(1024)S(1)} %bitcast.165, f32[3072]{0:T(1024)S(1)} %get-tuple-element.53), kind=kLoop, calls=%fused_computation.10 | loop fusion | flops 75497472 | bytes 75534336 | tf_op jit(solution)/shard_map/convert_element_type | solution.py:55
  366.4 114.0 %convolution_reduce-precision_fusion.2 = f32[3072,4096]{1,0:T(8,128)} fusion(bf16[3072,4096]{1,0:T(8,128)(2,1)} %multiply_convert_fusion.2, bf16[4096,4096]{1,0:T(8,128)(2,1)} %param.9), kind=kOutput, calls=%fused_computation.15 | convolution fusion | flops 103091798016 | bytes 109051904 | tf_op jit(solution)/shard_map/dot_general | solution.py:58
  480.7 154.6 %fusion.70 = (f32[4096]{0:T(1024)S(1)}, f32[4096,4096]{0,1:T(8,128)}) fusion(bf16[4096,4096]{1,0:T(8,128)(2,1)} %all-gather.18.cloned.1.call-done, bf16[4096,4096]{1,0:T(8,128)(2,1)} %param.9), kind=kOutput, calls=%fused_computation.152 | convolution fusion | flops 137455730688 | bytes 134234112 | tf_op jit(solution)/shard_map/dot_general | solution.py:45
  635.3 21.8 %select_reduce_fusion.1 = (f32[4096]{0:T(1024)S(1)}, f32[4096]{0:T(1024)S(1)}) fusion(f32[4096,4096]{0,1:T(8,128)} %get-tuple-element.82, s32[4096]{0:T(1024)S(1)} %bitcast.162, f32[4096]{0:T(1024)S(1)} %get-tuple-element.81), kind=kLoop, calls=%fused_computation.2 | loop fusion | flops 83877888 | bytes 67174400 | tf_op jit(solution)/shard_map/reduce_sum | solution.py:48
  657.1 11.8 all-gather.7
  668.9 0.2 fusion.64
  669.3 0.6 fusion.59
  669.9 33.7 %multiply_convert_fusion.1 = bf16[4096,4096]{0,1:T(8,128)(2,1)} fusion(f32[4096,4096]{0,1:T(8,128)} %get-tuple-element.82, f32[4096]{0:T(1024)S(1)} %bitcast.167, s32[4096]{0:T(1024)S(1)} %bitcast.163, f32[4096]{0:T(1024)S(1)} %get-tuple-element.49), kind=kLoop, calls=%fused_computation.6 | loop fusion | flops 100663296 | bytes 100712448 | tf_op jit(solution)/shard_map/convert_element_type | solution.py:55
  703.7 149.7 %convolution_reduce-precision_fusion.1 = f32[4096,4096]{1,0:T(8,128)} fusion(bf16[4096,4096]{0,1:T(8,128)(2,1)} %multiply_convert_fusion.1, bf16[4096,4096]{1,0:T(8,128)(2,1)} %param.9), kind=kOutput, calls=%fused_computation.14 | convolution fusion | flops 137455730688 | bytes 134217728 | tf_op jit(solution)/shard_map/dot_general | solution.py:58
  853.5 0.3 reduce-scatter.11.cloned.1.call-start
  853.8 0.4 copy-done.1
  854.1 3.1 fusion.33
  857.3 2.4 fusion.34
  859.6 6.4 dynamic_update_slice.12
  867.3 154.6 %fusion.71 = (f32[4096]{0:T(1024)S(1)}, f32[4096,4096]{0,1:T(8,128)}) fusion(bf16[4096,4096]{1,0:T(8,128)(2,1)} %all-gather.20.cloned.1.call-done, bf16[4096,4096]{1,0:T(8,128)(2,1)} %param.9), kind=kOutput, calls=%fused_computation.153 | convolution fusion | flops 137455730688 | bytes 134234112 | tf_op jit(solution)/shard_map/dot_general | solution.py:45
  1021.9 21.8 %select_reduce_fusion = (f32[4096]{0:T(1024)S(1)}, f32[4096]{0:T(1024)S(1)}) fusion(f32[4096,4096]{0,1:T(8,128)} %get-tuple-element.84, s32[4096]{0:T(1024)S(1)} %bitcast.160, f32[4096]{0:T(1024)S(1)} %get-tuple-element.83), kind=kLoop, calls=%fused_computation.1 | loop fusion | flops 83877888 | bytes 67174400 | tf_op jit(solution)/shard_map/reduce_sum | solution.py:48
  1043.8 13.9 all-gather.8
  1057.6 0.2 fusion.63
  1058.1 1.4 fusion.52
  1059.5 33.7 %multiply_convert_fusion = bf16[4096,4096]{0,1:T(8,128)(2,1)} fusion(f32[4096,4096]{0,1:T(8,128)} %get-tuple-element.84, f32[4096]{0:T(1024)S(1)} %bitcast.166, s32[4096]{0:T(1024)S(1)} %bitcast.161, f32[4096]{0:T(1024)S(1)} %get-tuple-element.51), kind=kLoop, calls=%fused_computation.3 | loop fusion | flops 100663296 | bytes 100712448 | tf_op jit(solution)/shard_map/convert_element_type | solution.py:55
  1093.2 149.8 %convolution_reduce-precision_fusion = f32[4096,4096]{1,0:T(8,128)} fusion(bf16[4096,4096]{0,1:T(8,128)(2,1)} %multiply_convert_fusion, bf16[4096,4096]{1,0:T(8,128)(2,1)} %param.9), kind=kOutput, calls=%fused_computation.13 | convolution fusion | flops 137455730688 | bytes 134217728 | tf_op jit(solution)/shard_map/dot_general | solution.py:58
  1244.3 116.7 %fusion.72 = f32[4096,4096]{1,0:T(8,128)} fusion(bf16[3072,4096]{1,0:T(8,128)(2,1)} %all-gather.16.cloned.1.call-done, bf16[3072,4096]{1,0:T(8,128)(2,1)} %multiply_convert_fusion.2), kind=kOutput, calls=%fused_computation.154 | convolution fusion | flops 103079215104 | bytes 117440512 | tf_op jit(solution)/shard_map/dot_general | solution.py:64
  1361.1 149.7 %fusion.73 = f32[4096,4096]{1,0:T(8,128)} fusion(bf16[4096,4096]{1,0:T(8,128)(2,1)} %all-gather.18.cloned.1.call-done, bf16[4096,4096]{0,1:T(8,128)(2,1)} %multiply_convert_fusion.1), kind=kOutput, calls=%fused_computation.155 | convolution fusion | flops 137438953472 | bytes 134217728 | tf_op jit(solution)/shard_map/dot_general | solution.py:64
  1510.8 150.1 %fusion.74 = f32[4096,4096]{1,0:T(8,128)} fusion(bf16[4096,4096]{1,0:T(8,128)(2,1)} %all-gather.20.cloned.1.call-done, bf16[4096,4096]{0,1:T(8,128)(2,1)} %multiply_convert_fusion), kind=kOutput, calls=%fused_computation.156 | convolution fusion | flops 137438953472 | bytes 134217728 | tf_op jit(solution)/shard_map/dot_general | solution.py:64
  1660.9 79.3 %add_convert_fusion = bf16[4096,4096]{1,0:T(8,128)(2,1)} fusion(f32[4096,4096]{1,0:T(8,128)} %fusion.74, f32[4096,4096]{1,0:T(8,128)} %fusion.73, f32[4096,4096]{1,0:T(8,128)} %fusion.72, bf16[1024,4096]{1,0:T(8,128)(2,1)} %all-gather.14.cloned.1.call-done, bf16[1024,4096]{1,0:T(8,128)(2,1)} %multiply_convert_fusion.3), kind=kOutput, calls=%fused_computation | convolution fusion | flops 34426847232 | bytes 251658240 | tf_op jit(solution)/shard_map/dot_general | solution.py:64
  1740.2 4.7 fusion.20
  1745.0 5.7 fusion.26
  1750.7 11.6 fusion.13
  1762.3 22.6 %psum.7 = f32[4224]{0:T(1024)S(1)} all-reduce(f32[4224]{0:T(1024)S(1)} %concatenate.3), channel_id=1, replica_groups=mesh['tp'=8] {'tp'}, use_global_device_ids=true, to_apply=%region_37.38 | all-reduce | flops 4224 | bytes 33792 | tf_op jit(solution)/shard_map/psum | solution.py:73
  1785.0 0.7 slice_reduce_fusion
  1785.7 0.6 slice.119
  1787.7 7.3 fusion.24
  1795.0 1.3 slice-done.1
  1796.3 5.5 fusion.22
  (105 shorter events, 1.7 us)
Async XLA Ops:
  7.2 18.6 %copy-start = (f32[4096]{0:T(1024)S(1)}, f32[4096]{0:T(1024)}, u32[]{:S(2)}) copy-start(f32[4096]{0:T(1024)} %param.8) | copy-start | bytes 49156
  7.2 57.3 %all-gather.14.cloned.1.call-start = ((), (), s32[]{:S(2)}) async-start(), calls=%async_computation.4 | async-start | bytes 9437184 | tf_op jit(solution)/shard_map/all_gather | solution.py:27
  8.7 0.5 copy-start.29
  9.3 0.5 copy-start.27
  12.4 174.4 %all-gather.16.cloned.1.call-start = ((), (), s32[]{:S(2)}) async-start(), calls=%async_computation.6 | async-start | bytes 28311552 | tf_op jit(solution)/shard_map/all_gather | solution.py:27
  15.0 0.6 copy-start.19
  15.6 0.5 copy-start.13
  20.7 12.4 copy-start.25
  20.7 12.4 copy-start.26
  20.7 459.9 %all-gather.18.cloned.1.call-start = ((), (), s32[]{:S(2)}) async-start(), calls=%async_computation.8 | async-start | bytes 37748736 | tf_op jit(solution)/shard_map/all_gather | solution.py:27
  25.2 0.6 copy-start.21
  25.2 0.6 copy-start.23
  25.8 7.2 copy-start.17
  25.8 7.2 copy-start.15
  33.0 820.7 %reduce-scatter.5.cloned.1.call-start = ((), (), s32[]{:S(2)}) async-start(), calls=%async_computation.5 | async-start | bytes 18874368 | tf_op jit(solution)/shard_map/reduce_scatter | solution.py:60
  48.2 130.6 %copy-start.3 = (s32[8,3,512]{2,1,0:T(4,128)}, s32[8,3,512]{2,1,0:T(4,128)S(1)}, u32[]{:S(2)}) copy-start(s32[8,3,512]{2,1,0:T(4,128)S(1)} %fusion.45) | copy-start | bytes 147460
  48.9 128.6 %copy-start.5 = (f32[8,3,512]{2,1,0:T(4,128)}, f32[8,3,512]{2,1,0:T(4,128)S(1)}, u32[]{:S(2)}) copy-start(f32[8,3,512]{2,1,0:T(4,128)S(1)} %fusion.47) | copy-start | bytes 147460
  176.0 691.2 %all-gather.20.cloned.1.call-start = ((), (), s32[]{:S(2)}) async-start(), calls=%async_computation.10 | async-start | bytes 37748736 | tf_op jit(solution)/shard_map/all_gather | solution.py:27
  176.6 1563.6 %reduce-scatter.7.cloned.1.call-start = ((), (), s32[]{:S(2)}) async-start(), calls=%async_computation.7 | async-start | bytes 56623104 | tf_op jit(solution)/shard_map/reduce_scatter | solution.py:60
  186.8 114.3 %copy-start.9 = (s32[8,1,384]{2,1,0:T(1,128)S(1)}, s32[8,1,384]{2,1,0:T(1,128)}, u32[]{:S(2)}) copy-start(s32[8,1,384]{2,1,0:T(1,128)} %slice.108) | copy-start | bytes 36868
  480.4 1270.3 %reduce-scatter.9.cloned.1.call-start = ((), (), s32[]{:S(2)}) async-start(), calls=%async_computation.9 | async-start | bytes 75497472 | tf_op jit(solution)/shard_map/reduce_scatter | solution.py:60
  480.7 154.6 %copy-start.8 = (s32[8,1,512]{2,1,0:T(1,128)S(1)}, s32[8,1,512]{2,1,0:T(1,128)}, u32[]{:S(2)}) copy-start(s32[8,1,512]{2,1,0:T(1,128)} %get-tuple-element.73) | copy-start | bytes 49156
  635.3 34.6 %copy-start.11 = (f32[8,1,512]{2,1,0:T(1,128)S(1)}, f32[8,1,512]{2,1,0:T(1,128)}, u32[]{:S(2)}) copy-start(f32[8,1,512]{2,1,0:T(1,128)} %slice_divide_fusion.1) | copy-start | bytes 49156
  853.4 0.7 copy-start.1
  853.4 0.7 copy-start.28
  853.4 3.8 copy-start.30
  853.5 897.2 %reduce-scatter.11.cloned.1.call-start = ((), (), s32[]{:S(2)}) async-start(), calls=%async_computation.11 | async-start | bytes 75497472 | tf_op jit(solution)/shard_map/reduce_scatter | solution.py:60
  867.3 154.6 %copy-start.7 = (s32[8,1,512]{2,1,0:T(1,128)S(1)}, s32[8,1,512]{2,1,0:T(1,128)}, u32[]{:S(2)}) copy-start(s32[8,1,512]{2,1,0:T(1,128)} %get-tuple-element.72) | copy-start | bytes 49156
  1021.9 36.2 %copy-start.4 = (s32[8,3,512]{2,1,0:T(4,128)S(1)}, s32[8,3,512]{2,1,0:T(4,128)}, u32[]{:S(2)}) copy-start(s32[8,3,512]{2,1,0:T(4,128)} %copy-done.3) | copy-start | bytes 147460
  1021.9 36.2 %copy-start.6 = (f32[8,3,512]{2,1,0:T(4,128)S(1)}, f32[8,3,512]{2,1,0:T(4,128)}, u32[]{:S(2)}) copy-start(f32[8,3,512]{2,1,0:T(4,128)} %copy-done.5) | copy-start | bytes 147460
  1021.9 36.2 %copy-start.12 = (f32[4096]{0:T(1024)S(1)}, f32[4096]{0:T(1024)}, u32[]{:S(2)}) copy-start(f32[4096]{0:T(1024)} %get-tuple-element.48) | copy-start | bytes 49156
  1660.9 79.3 %copy-start.2 = (f32[4096]{0:T(1024)S(1)}, f32[4096]{0:T(1024)}, u32[]{:S(2)}) copy-start(f32[4096]{0:T(1024)} %param.8) | copy-start | bytes 49156
  1660.9 79.4 %copy-start.14 = (f32[384]{0:T(512)S(1)}, f32[384]{0:T(512)}, u32[]{:S(2)}) copy-start(f32[384]{0:T(512)} %copy-done.13) | copy-start | bytes 4612
  1660.9 84.0 %copy-start.20 = (f32[384]{0:T(512)S(1)}, f32[384]{0:T(512)}, u32[]{:S(2)}) copy-start(f32[384]{0:T(512)} %copy-done.19) | copy-start | bytes 4612
  1740.2 10.5 copy-start.16
  1740.2 10.5 copy-start.18
  1744.9 17.4 copy-start.10
  1744.9 42.7 %copy-start.22 = (f32[512]{0:T(512)S(1)}, f32[512]{0:T(512)}, u32[]{:S(2)}) copy-start(f32[512]{0:T(512)} %copy-done.21) | copy-start | bytes 6148
  1744.9 42.7 %copy-start.24 = (f32[512]{0:T(512)S(1)}, f32[512]{0:T(512)}, u32[]{:S(2)}) copy-start(f32[512]{0:T(512)} %copy-done.23) | copy-start | bytes 6148
  1787.7 7.3 slice-start
  1787.7 8.6 slice-start.1
Sparse Core Ops, SparseCore 0:
  12.5 51.9 all-gather.13
  66.3 120.4 all-gather.15
  189.2 156.4 all-gather.17
  349.6 106.9 reduce-scatter.4
  458.3 155.2 all-gather.19
  616.9 274.5 reduce-scatter.6
  895.0 376.3 reduce-scatter.8
  1274.8 374.7 reduce-scatter.10

commit v3 on v2

--- a/solution.py
+++ b/solution.py
@@ -59,9 +59,10 @@
             part = lax.reduce_precision(part, 8, 7)
             reduced.append(lax.psum_scatter(part, 'tp', scatter_dimension=0, tiled=True))
         hn_late, dz_late, _ = lax.optimization_barrier((hn, d_logits, part))
-        d_head = jnp.zeros((), f32)
+        d_head = None
         for h, dz in zip(hn_late, dz_late):
-            d_head = d_head + lax.dot_general(h, dz, (((0,), (0,)), ((), ())), preferred_element_type=f32)
+            term = lax.dot_general(h, dz, (((0,), (0,)), ((), ())), preferred_element_type=f32)
+            d_head = term if d_head is None else lax.optimization_barrier(d_head) + term
         d_head = d_head.astype(jnp.bfloat16)
 
         d_x, d_gain = [], jnp.zeros((model_width,), f32)
@@ -70,7 +71,7 @@
             d_x_i, d_gain_i = norm_vjp(d_norm)
             d_x.append(d_x_i.astype(jnp.bfloat16))
             d_gain = d_gain + d_gain_i
-        tail = lax.psum(jnp.concatenate([d_gain, jnp.full((128,), loss_part / 128.0)]), 'tp')
+        tail = jnp.sum(lax.all_gather(jnp.concatenate([d_gain, jnp.full((128,), loss_part / 128.0)]), 'tp', axis=0), axis=0)
         mean_loss = jnp.sum(tail[model_width:]) / kept_count
         d_hidden = jnp.zeros(hidden.shape, jnp.bfloat16)
         for (b, lo, hi), d_x_i in zip(chunks, d_x):

time: 1820 us -> 1790 us (0.984)
  matrix products: 1420 us -> 1400 us
    psum x1 -> x0, blocking collectives: 22.6 us -> none  [device_step(): lax.psum(jnp.concatenate([d_gain, jnp.full((128,), loss_part / 128.0)]),...]
where the time goes in v3:
time: 1790 us
  matrix products  1400 us (78%)
  other arithmetic  247 us (14%)
  blocking collectives  77 us (4%)
  waiting for transfers between devices  23.9 us (1%)
  between operations  20.2 us (1%)
    dot_general x4, matrix products, device_step(): lax.dot_general(h, dz, (((0,), (0,)), ((), ())), preferred_element_type=f32)  483 us
    dot_general x4, matrix products, device_step(): z = jnp.dot(h, w_head, preferred_element_type=f32)  465 us
    dot_general x4, matrix products, device_step(): lax.dot_general(dz, w_head, (((1,), (1,)), ((), ())), preferred_element_t...  457 us
    convert_element_type x4, other arithmetic, device_step(): ((jnp.exp(z - log_norm[:, None]) - is_label) * (tok_weight / kept_count)[...  101 us
    reduce_sum x4, other arithmetic, device_step(): picked = jnp.sum(jnp.where(col_ids == loc_label[:, None], z, 0.0), axis=-1)  73.1 us
    all_gather x4, blocking collectives, device_step(): stats = lax.all_gather(jnp.stack([m, s]), 'tp', axis=0)  50.4 us
  transfers between devices with their start and end apart: 8, of which 2 were waited for; matrix products, arithmetic and copies ran while one was open for 91% of the time, Pallas kernels for 0%

profile of v3, /device:TPU:0, one launch (start us, length us, event | category | flops | bytes accessed | tf_op | source)
XLA Modules:
  0.0 1786.4 jit_solution(3789467883989060497)
XLA Ops:
  7.2 1.5 fusion.32
  8.7 0.6 copy-done.30
  9.3 0.5 copy-done.28
  9.8 2.6 fusion.29
  12.5 2.6 fusion.19
  15.1 0.5 copy-done.20
  15.7 0.6 copy-done.14
  16.3 4.6 fusion.16
  21.0 4.4 fusion.10
  25.4 0.5 copy-done.24
  26.0 7.2 fusion.6
  33.3 15.5 all-gather.1
  48.8 0.6 fusion.46
  49.5 15.1 all-gather.16.cloned.1.call-done
  64.6 41.3 %fusion.68 = (f32[1024]{0:T(1024)S(1)}, f32[1024,4096]{1,0:T(8,128)S(1)}) fusion(bf16[1024,4096]{1,0:T(8,128)(2,1)} %all-gather.16.cloned.1.call-done, bf16[4096,4096]{1,0:T(8,128)(2,1)} %param.9), kind=kOutput, calls=%fused_computation.152 | convolution fusion | flops 34363932672 | bytes 58724352 | tf_op jit(solution)/shard_map/dot_general | solution.py:45
  106.0 5.6 select_reduce_fusion.3
  111.6 12.0 all-gather.6
  123.7 1.3 fusion.54
  125.1 7.9 multiply_convert_fusion.3
  133.0 43.1 %convolution_reduce-precision_fusion.3 = f32[1024,4096]{1,0:T(8,128)} fusion(bf16[1024,4096]{1,0:T(8,128)(2,1)} %multiply_convert_fusion.3, bf16[4096,4096]{1,0:T(8,128)(2,1)} %param.9), kind=kOutput, calls=%fused_computation.41 | convolution fusion | flops 34363932672 | bytes 58720256 | tf_op jit(solution)/shard_map/dot_general | solution.py:58
  176.1 0.5 all-gather.22.cloned.1.call-update
  176.7 0.3 reduce-scatter.7.cloned.1.call-start
  176.9 0.6 slice.108
  177.5 1.3 slice_divide_fusion.1
  178.8 0.6 fusion.66
  179.4 8.1 all-gather.18.cloned.1.call-done
  187.5 114.3 %fusion.69 = (f32[3072]{0:T(1024)S(1)}, f32[3072,4096]{1,0:T(8,128)}) fusion(bf16[3072,4096]{1,0:T(8,128)(2,1)} %all-gather.18.cloned.1.call-done, bf16[4096,4096]{1,0:T(8,128)(2,1)} %param.9), kind=kOutput, calls=%fused_computation.153 | convolution fusion | flops 103091798016 | bytes 109064192 | tf_op jit(solution)/shard_map/dot_general | solution.py:45
  301.8 24.0 %select_reduce_fusion.2 = (f32[3072]{0:T(1024)S(1)}, f32[3072]{0:T(1024)S(1)}) fusion(f32[3072,4096]{1,0:T(8,128)} %get-tuple-element.80, s32[3072]{0:T(1024)S(1)} %bitcast.162, f32[3072]{0:T(1024)S(1)} %get-tuple-element.79), kind=kLoop, calls=%fused_computation.9 | loop fusion | flops 62908416 | bytes 50380800 | tf_op jit(solution)/shard_map/reduce_sum | solution.py:48
  325.8 12.8 all-gather.7
  338.9 2.2 fusion.53
  341.1 25.9 %multiply_convert_fusion.2 = bf16[3072,4096]{1,0:T(8,128)(2,1)} fusion(f32[3072,4096]{1,0:T(8,128)} %get-tuple-element.80, f32[3072]{0:T(1024)S(1)} %bitcast.174, s32[3072]{0:T(1024)S(1)} %bitcast.163, f32[3072]{0:T(1024)S(1)} %get-tuple-element.53), kind=kLoop, calls=%fused_computation.10 | loop fusion | flops 75497472 | bytes 75534336 | tf_op jit(solution)/shard_map/convert_element_type | solution.py:55
  367.0 114.0 %convolution_reduce-precision_fusion.2 = f32[3072,4096]{1,0:T(8,128)} fusion(bf16[3072,4096]{1,0:T(8,128)(2,1)} %multiply_convert_fusion.2, bf16[4096,4096]{1,0:T(8,128)(2,1)} %param.9), kind=kOutput, calls=%fused_computation.17 | convolution fusion | flops 103091798016 | bytes 109051904 | tf_op jit(solution)/shard_map/dot_general | solution.py:58
  481.0 0.5 reduce-scatter.9.cloned.1.call-start
  481.5 154.6 %fusion.70 = (f32[4096]{0:T(1024)S(1)}, f32[4096,4096]{0,1:T(8,128)}) fusion(bf16[4096,4096]{1,0:T(8,128)(2,1)} %all-gather.20.cloned.1.call-done, bf16[4096,4096]{1,0:T(8,128)(2,1)} %param.9), kind=kOutput, calls=%fused_computation.154 | convolution fusion | flops 137455730688 | bytes 134234112 | tf_op jit(solution)/shard_map/dot_general | solution.py:45
  636.2 21.8 %select_reduce_fusion.1 = (f32[4096]{0:T(1024)S(1)}, f32[4096]{0:T(1024)S(1)}) fusion(f32[4096,4096]{0,1:T(8,128)} %get-tuple-element.82, s32[4096]{0:T(1024)S(1)} %bitcast.160, f32[4096]{0:T(1024)S(1)} %get-tuple-element.81), kind=kLoop, calls=%fused_computation.2 | loop fusion | flops 83877888 | bytes 67174400 | tf_op jit(solution)/shard_map/reduce_sum | solution.py:48
  658.0 11.7 all-gather.8
  669.7 0.2 fusion.64
  670.1 0.6 fusion.59
  670.8 33.7 %multiply_convert_fusion.1 = bf16[4096,4096]{0,1:T(8,128)(2,1)} fusion(f32[4096,4096]{0,1:T(8,128)} %get-tuple-element.82, f32[4096]{0:T(1024)S(1)} %bitcast.165, s32[4096]{0:T(1024)S(1)} %bitcast.161, f32[4096]{0:T(1024)S(1)} %get-tuple-element.49), kind=kLoop, calls=%fused_computation.6 | loop fusion | flops 100663296 | bytes 100712448 | tf_op jit(solution)/shard_map/convert_element_type | solution.py:55
  704.4 149.7 %convolution_reduce-precision_fusion.1 = f32[4096,4096]{1,0:T(8,128)} fusion(bf16[4096,4096]{0,1:T(8,128)(2,1)} %multiply_convert_fusion.1, bf16[4096,4096]{1,0:T(8,128)(2,1)} %param.9), kind=kOutput, calls=%fused_computation.14 | convolution fusion | flops 137455730688 | bytes 134217728 | tf_op jit(solution)/shard_map/dot_general | solution.py:58
  854.2 0.3 reduce-scatter.11.cloned.1.call-start
  854.5 0.4 copy-done.2
  854.9 3.1 fusion.33
  858.0 2.4 fusion.34
  860.4 6.4 dynamic_update_slice.12
  868.2 154.6 %fusion.71 = (f32[4096]{0:T(1024)S(1)}, f32[4096,4096]{0,1:T(8,128)}) fusion(bf16[4096,4096]{1,0:T(8,128)(2,1)} %all-gather.22.cloned.1.call-done, bf16[4096,4096]{1,0:T(8,128)(2,1)} %param.9), kind=kOutput, calls=%fused_computation.155 | convolution fusion | flops 137455730688 | bytes 134234112 | tf_op jit(solution)/shard_map/dot_general | solution.py:45
  1022.8 21.8 %select_reduce_fusion = (f32[4096]{0:T(1024)S(1)}, f32[4096]{0:T(1024)S(1)}) fusion(f32[4096,4096]{0,1:T(8,128)} %get-tuple-element.84, s32[4096]{0:T(1024)S(1)} %bitcast.158, f32[4096]{0:T(1024)S(1)} %get-tuple-element.83), kind=kLoop, calls=%fused_computation.1 | loop fusion | flops 83877888 | bytes 67174400 | tf_op jit(solution)/shard_map/reduce_sum | solution.py:48
  1044.7 13.8 all-gather.9
  1059.0 1.3 fusion.52
  1060.3 33.7 %multiply_convert_fusion = bf16[4096,4096]{0,1:T(8,128)(2,1)} fusion(f32[4096,4096]{0,1:T(8,128)} %get-tuple-element.84, f32[4096]{0:T(1024)S(1)} %bitcast.164, s32[4096]{0:T(1024)S(1)} %bitcast.159, f32[4096]{0:T(1024)S(1)} %get-tuple-element.51), kind=kLoop, calls=%fused_computation.3 | loop fusion | flops 100663296 | bytes 100712448 | tf_op jit(solution)/shard_map/convert_element_type | solution.py:55
  1094.0 149.8 %convolution_reduce-precision_fusion = f32[4096,4096]{1,0:T(8,128)} fusion(bf16[4096,4096]{0,1:T(8,128)(2,1)} %multiply_convert_fusion, bf16[4096,4096]{1,0:T(8,128)(2,1)} %param.9), kind=kOutput, calls=%fused_computation.13 | convolution fusion | flops 137455730688 | bytes 134217728 | tf_op jit(solution)/shard_map/dot_general | solution.py:58
  1243.8 46.2 %fusion.72 = f32[4096,4096]{1,0:T(8,128)} fusion(bf16[1024,4096]{1,0:T(8,128)(2,1)} %all-gather.16.cloned.1.call-done, bf16[1024,4096]{1,0:T(8,128)(2,1)} %multiply_convert_fusion.3), kind=kOutput, calls=%fused_computation.156 | convolution fusion | flops 34359738368 | bytes 83886080 | tf_op jit(solution)/shard_map/dot_general | solution.py:64
  1290.0 121.7 %convolution_add_fusion.1 = f32[4096,4096]{1,0:T(8,128)} fusion(f32[4096,4096]{1,0:T(8,128)} %fusion.72, bf16[3072,4096]{1,0:T(8,128)(2,1)} %all-gather.18.cloned.1.call-done, bf16[3072,4096]{1,0:T(8,128)(2,1)} %multiply_convert_fusion.2), kind=kOutput, calls=%fused_computation.16 | convolution fusion | flops 103095992320 | bytes 184549376 | tf_op jit(solution)/shard_map/dot_general | solution.py:64
  1411.7 159.2 %convolution_add_fusion = f32[4096,4096]{1,0:T(8,128)} fusion(f32[4096,4096]{1,0:T(8,128)} %convolution_add_fusion.1, bf16[4096,4096]{1,0:T(8,128)(2,1)} %all-gather.20.cloned.1.call-done, bf16[4096,4096]{0,1:T(8,128)(2,1)} %multiply_convert_fusion.1), kind=kOutput, calls=%fused_computation.15 | convolution fusion | flops 137455730688 | bytes 201326592 | tf_op jit(solution)/shard_map/dot_general | solution.py:64
  1572.1 155.8 %add_convert_fusion = bf16[4096,4096]{1,0:T(8,128)(2,1)} fusion(f32[4096,4096]{1,0:T(8,128)} %convolution_add_fusion, bf16[4096,4096]{1,0:T(8,128)(2,1)} %all-gather.22.cloned.1.call-done, bf16[4096,4096]{0,1:T(8,128)(2,1)} %multiply_convert_fusion), kind=kOutput, calls=%fused_computation | convolution fusion | flops 137472507904 | bytes 167772160 | tf_op jit(solution)/shard_map/dot_general | solution.py:64
  1727.9 4.7 fusion.20
  1732.6 5.7 fusion.26
  1738.3 11.6 fusion.13
  1750.0 11.1 all-gather.10
  1761.3 0.7 slice_reduce_fusion
  1761.9 0.6 slice.119
  1763.9 7.6 fusion.24
  1771.5 1.0 copy-done
  1772.5 5.5 fusion.22
  (105 shorter events, 1.9 us)
Async XLA Ops:
  7.2 18.8 %copy-start.1 = (f32[4096]{0:T(1024)S(1)}, f32[4096]{0:T(1024)}, u32[]{:S(2)}) copy-start(f32[4096]{0:T(1024)} %param.8) | copy-start | bytes 49156
  7.2 57.4 %all-gather.16.cloned.1.call-start = ((), (), s32[]{:S(2)}) async-start(), calls=%async_computation.4 | async-start | bytes 9437184 | tf_op jit(solution)/shard_map/all_gather | solution.py:27
  8.7 0.6 copy-start.30
  9.3 0.5 copy-start.28
  12.5 175.0 %all-gather.18.cloned.1.call-start = ((), (), s32[]{:S(2)}) async-start(), calls=%async_computation.6 | async-start | bytes 28311552 | tf_op jit(solution)/shard_map/all_gather | solution.py:27
  15.1 0.5 copy-start.20
  15.7 0.6 copy-start.14
  20.9 12.4 copy-start.26
  20.9 12.4 copy-start.27
  20.9 460.6 %all-gather.20.cloned.1.call-start = ((), (), s32[]{:S(2)}) async-start(), calls=%async_computation.8 | async-start | bytes 37748736 | tf_op jit(solution)/shard_map/all_gather | solution.py:27
  25.4 0.6 copy-start.24
  25.4 0.6 copy-start.22
  25.9 7.3 copy-start.18
  26.0 7.2 copy-start.16
  33.2 821.3 %reduce-scatter.5.cloned.1.call-start = ((), (), s32[]{:S(2)}) async-start(), calls=%async_computation.5 | async-start | bytes 18874368 | tf_op jit(solution)/shard_map/reduce_scatter | solution.py:60
  48.8 130.0 %copy-start.4 = (s32[8,3,512]{2,1,0:T(4,128)}, s32[8,3,512]{2,1,0:T(4,128)S(1)}, u32[]{:S(2)}) copy-start(s32[8,3,512]{2,1,0:T(4,128)S(1)} %fusion.45) | copy-start | bytes 147460
  49.5 128.1 %copy-start.6 = (f32[8,3,512]{2,1,0:T(4,128)}, f32[8,3,512]{2,1,0:T(4,128)S(1)}, u32[]{:S(2)}) copy-start(f32[8,3,512]{2,1,0:T(4,128)S(1)} %fusion.47) | copy-start | bytes 147460
  176.1 692.1 %all-gather.22.cloned.1.call-start = ((), (), s32[]{:S(2)}) async-start(), calls=%async_computation.10 | async-start | bytes 37748736 | tf_op jit(solution)/shard_map/all_gather | solution.py:27
  176.7 1551.2 %reduce-scatter.7.cloned.1.call-start = ((), (), s32[]{:S(2)}) async-start(), calls=%async_computation.7 | async-start | bytes 56623104 | tf_op jit(solution)/shard_map/reduce_scatter | solution.py:60
  187.5 114.3 %copy-start.10 = (s32[8,1,384]{2,1,0:T(1,128)S(1)}, s32[8,1,384]{2,1,0:T(1,128)}, u32[]{:S(2)}) copy-start(s32[8,1,384]{2,1,0:T(1,128)} %slice.108) | copy-start | bytes 36868
  481.0 1257.3 %reduce-scatter.9.cloned.1.call-start = ((), (), s32[]{:S(2)}) async-start(), calls=%async_computation.9 | async-start | bytes 75497472 | tf_op jit(solution)/shard_map/reduce_scatter | solution.py:60
  481.5 154.6 %copy-start.9 = (s32[8,1,512]{2,1,0:T(1,128)S(1)}, s32[8,1,512]{2,1,0:T(1,128)}, u32[]{:S(2)}) copy-start(s32[8,1,512]{2,1,0:T(1,128)} %get-tuple-element.73) | copy-start | bytes 49156
  636.2 34.6 %copy-start.12 = (f32[8,1,512]{2,1,0:T(1,128)S(1)}, f32[8,1,512]{2,1,0:T(1,128)}, u32[]{:S(2)}) copy-start(f32[8,1,512]{2,1,0:T(1,128)} %slice_divide_fusion.1) | copy-start | bytes 49156
  854.2 0.7 copy-start.2
  854.2 0.7 copy-start.29
  854.2 3.8 copy-start.31
  854.2 884.1 %reduce-scatter.11.cloned.1.call-start = ((), (), s32[]{:S(2)}) async-start(), calls=%async_computation.11 | async-start | bytes 75497472 | tf_op jit(solution)/shard_map/reduce_scatter | solution.py:60
  868.2 154.6 %copy-start.8 = (s32[8,1,512]{2,1,0:T(1,128)S(1)}, s32[8,1,512]{2,1,0:T(1,128)}, u32[]{:S(2)}) copy-start(s32[8,1,512]{2,1,0:T(1,128)} %get-tuple-element.72) | copy-start | bytes 49156
  1022.8 36.1 %copy-start.5 = (s32[8,3,512]{2,1,0:T(4,128)S(1)}, s32[8,3,512]{2,1,0:T(4,128)}, u32[]{:S(2)}) copy-start(s32[8,3,512]{2,1,0:T(4,128)} %copy-done.4) | copy-start | bytes 147460
  1022.8 36.2 %copy-start.7 = (f32[8,3,512]{2,1,0:T(4,128)S(1)}, f32[8,3,512]{2,1,0:T(4,128)}, u32[]{:S(2)}) copy-start(f32[8,3,512]{2,1,0:T(4,128)} %copy-done.6) | copy-start | bytes 147460
  1022.8 36.2 %copy-start.13 = (f32[4096]{0:T(1024)S(1)}, f32[4096]{0:T(1024)}, u32[]{:S(2)}) copy-start(f32[4096]{0:T(1024)} %get-tuple-element.48) | copy-start | bytes 49156
  1572.1 155.8 %copy-start.3 = (f32[4096]{0:T(1024)S(1)}, f32[4096]{0:T(1024)}, u32[]{:S(2)}) copy-start(f32[4096]{0:T(1024)} %param.8) | copy-start | bytes 49156
  1572.1 155.8 %copy-start.15 = (f32[384]{0:T(512)S(1)}, f32[384]{0:T(512)}, u32[]{:S(2)}) copy-start(f32[384]{0:T(512)} %copy-done.14) | copy-start | bytes 4612
  1572.1 160.5 %copy-start.21 = (f32[384]{0:T(512)S(1)}, f32[384]{0:T(512)}, u32[]{:S(2)}) copy-start(f32[384]{0:T(512)} %copy-done.20) | copy-start | bytes 4612
  1727.8 10.5 copy-start.17
  1727.8 10.5 copy-start.19
  1732.6 17.4 copy-start.11
  1732.6 30.0 %copy-start.25 = (f32[512]{0:T(512)S(1)}, f32[512]{0:T(512)}, u32[]{:S(2)}) copy-start(f32[512]{0:T(512)} %copy-done.24) | copy-start | bytes 6148
  1732.6 30.0 %copy-start.23 = (f32[512]{0:T(512)S(1)}, f32[512]{0:T(512)}, u32[]{:S(2)}) copy-start(f32[512]{0:T(512)} %copy-done.22) | copy-start | bytes 6148
  1763.9 8.6 copy-start
Sparse Core Ops, SparseCore 0:
  12.6 51.9 all-gather.15
  67.0 120.4 all-gather.17
  189.9 156.4 all-gather.19
  349.8 106.9 reduce-scatter.4
  458.4 155.2 all-gather.21
  617.0 274.5 reduce-scatter.6
  895.1 376.3 reduce-scatter.8
  1275.0 374.6 reduce-scatter.10
